TPU v7x, 256 devices: a whole 4x4x8 slice. The times are simulated.
256 devices in a mesh: dom: 256 (over y, z, x, core).
Axes of the slice: x: 4, y: 4, z: 8, core: 2. Of those that a mesh axis runs over, the one named last changes fastest.
Arguments:
- particles: bfloat16 [8192, 2, 7488], P('dom'), may hold values from -6 to 6
- references: bfloat16 [256, 2, 7488], P('dom'), may hold values from -6 to 6
- assignment: int32 [8192, 1], P('dom'), may hold values from 0 to 255
- orientation: int32 [8192], P('dom'), may hold values from 0 to 35
- tilt_range: int32 [2, 8192], P(None, 'dom'), may hold values from 0 to 20
Outputs:
- scores: float32 [8192, 256], P('dom')
- class_means: float32 [256, 2, 7488], P('dom')
- class_load: float32 [256], replicated
Inputs may be any that keep to these rules, and one draw needn't show every extreme that they name: `assignment`: every class has at least one particle.
All inputs are finite; a program needn't handle non-finite values.
Results may differ from a plain program's by a relative error of at most 0.0035.
Values may be sent and summed in bfloat16 or wider, within the bound.
A program may use at most 128 MiB of HBM per device.

v0:
```python
import math
import jax
import jax.numpy as jnp
from jax import lax
from jax.sharding import Mesh
from jax.sharding import PartitionSpec as P

GRID = 24
ORIENTS = 36
COEF = 7488
DOM = ("dom_0", "dom_1", "dom_2", "dom_3")
EPS = 1e-06
GAIN = 6.0
TAU = 0.5
member_rows = 256


def cut_along(shard, dim, size):
    before, after = (shard.shape[:dim], shard.shape[dim + 1 :])
    return jnp.moveaxis(shard.reshape(*before, size, -1, *after), dim, 0)


def summed_on_arrival(shard, axis, dim):
    tiles = cut_along(shard, dim, lax.axis_size(axis))
    arrived = lax.all_to_all(tiles, axis, split_axis=0, concat_axis=0, tiled=True)
    return arrived.astype(jnp.float32).sum(axis=0)


def sum_in_two_steps(shard, axes, dim):
    far, near = axes
    own = summed_on_arrival(cut_along(shard, dim, lax.axis_size(far)), near, dim + 1)
    return jnp.sum(
        lax.all_to_all(own.astype(jnp.bfloat16), far, 0, 0, tiled=True).astype(jnp.float32), axis=0
    )


def tables():
    index = jnp.arange(COEF, dtype=jnp.int32)
    plane = index // (GRID * GRID)
    rest = index % (GRID * GRID)
    col_x = rest // GRID
    col_z = rest % GRID
    freq_x = ((col_x + GRID // 2) % GRID - GRID // 2).astype(jnp.float32)
    freq_y = plane.astype(jnp.float32)
    freq_z = ((col_z + GRID // 2) % GRID - GRID // 2).astype(jnp.float32)
    return (freq_x, freq_y, freq_z)


def wedge_weights(orient, low_bin, high_bin):
    freq_x, freq_y, freq_z = tables()
    angle = orient.astype(jnp.float32) * (2.0 * math.pi / ORIENTS)
    along = -freq_x[None, :] * jnp.sin(angle)[:, None] + freq_y[None, :] * jnp.cos(angle)[:, None]
    radius = along * along + freq_z[None, :] * freq_z[None, :] + 1.0
    cos_two = (along * along - freq_z[None, :] * freq_z[None, :]) / radius
    sin_two = -2.0 * along * freq_z[None, :] / radius
    low = -(40.0 + 1.5 * low_bin.astype(jnp.float32)) * (math.pi / 180.0)
    high = (40.0 + 1.5 * high_bin.astype(jnp.float32)) * (math.pi / 180.0)
    centre = (low + high)[:, None]
    width = (high - low)[:, None]
    return jax.nn.sigmoid(
        GAIN * (cos_two * jnp.cos(centre) + sin_two * jnp.sin(centre) - jnp.cos(width))
    )


def body(particles, references, assignment, orientation, tilt_range):
    part_rows = particles.shape[0]
    coef = particles.shape[2]
    owned = references.shape[0]
    devices = lax.axis_size(DOM)
    classes = owned * devices
    total = part_rows * devices
    cls = assignment[:, 0]
    wedge = wedge_weights(orientation, tilt_range[0], tilt_range[1])
    pf = particles.astype(jnp.float32)
    weighted = (wedge[:, None, :] * pf).astype(jnp.bfloat16)
    flat = weighted.reshape(part_rows, 2 * coef)
    wedge_low = wedge.astype(jnp.bfloat16)
    power = jnp.sum(wedge * (pf[:, 0] * pf[:, 0] + pf[:, 1] * pf[:, 1]), axis=1)
    piece = lax.all_gather(references, DOM, axis=0, tiled=True)
    count = piece.shape[0]
    p32 = piece.astype(jnp.float32)
    ref_power = (p32[:, 0] * p32[:, 0] + p32[:, 1] * p32[:, 1]).astype(jnp.bfloat16)
    intersection = lax.dot_general(
        flat,
        piece.reshape(count, 2 * coef),
        (((1,), (1,)), ((), ())),
        preferred_element_type=jnp.float32,
    )
    energy = lax.dot_general(
        wedge_low, ref_power, (((1,), (1,)), ((), ())), preferred_element_type=jnp.float32
    )
    scores = intersection / (
        math.sqrt(coef) * jnp.sqrt((energy / coef + EPS) * (power[:, None] / coef + EPS))
    )
    ids = lax.iota(jnp.int32, owned * lax.axis_size(DOM))
    onehot = (ids[:, None] == cls[None, :]).astype(jnp.bfloat16)
    numer = sum_in_two_steps(
        jnp.dot(onehot, flat, preferred_element_type=jnp.float32).astype(jnp.bfloat16),
        (("dom_0", "dom_1"), ("dom_2", "dom_3")),
        0,
    )
    labels = jnp.stack([cls, orientation, tilt_range[0], tilt_range[1]])
    every = lax.all_gather(labels, DOM, axis=1, tiled=True)
    class_ids = jnp.arange(classes, dtype=jnp.int32)
    counts = jnp.sum((class_ids[:, None] == every[0][None, :]).astype(jnp.float32), axis=1)
    own_class = lax.axis_index(DOM) * owned + 0
    chosen = every[0] == own_class
    members = jnp.nonzero(chosen, size=total + member_rows, fill_value=0)[0].astype(jnp.int32)
    members_count = jnp.sum(chosen.astype(jnp.int32))
    block_count = (members_count + member_rows - 1) // member_rows

    def member_block(block, acc):
        square_sum, wedge_sum = acc
        first = (block * member_rows).astype(jnp.int32)
        picked = lax.dynamic_slice_in_dim(members, first, member_rows, 0)
        valid = (first + lax.iota(jnp.int32, member_rows) < members_count).astype(jnp.float32)
        member_wedge = wedge_weights(every[1][picked], every[2][picked], every[3][picked])
        squares = (member_wedge * member_wedge).astype(jnp.bfloat16).astype(jnp.float32)
        square_sum = square_sum + jnp.sum(valid[:, None] * squares, axis=0)
        wedge_sum = wedge_sum + jnp.sum(valid * jnp.sum(member_wedge, axis=1))
        return (square_sum, wedge_sum)

    square_sum, wedge_sum = lax.fori_loop(
        0, block_count, member_block, (jnp.zeros((coef,), jnp.float32), jnp.zeros((), jnp.float32))
    )
    denom_rows = [square_sum]
    total_rows = [wedge_sum]
    denom = jnp.stack(denom_rows)
    own_totals = jnp.stack(total_rows)
    bottom = denom + TAU * (own_totals[:, None] / coef + 1.0)
    class_means = numer.reshape(owned, 2, coef) / bottom[:, None, :]
    class_load = counts * classes / total
    return (scores, class_means, class_load)


def solution(mesh):
    split = Mesh(mesh.devices.reshape(4, 8, 4, 2), ("dom_0", "dom_1", "dom_2", "dom_3"))
    placed = (P(DOM, None, None), P(DOM, None, None), P(DOM, None), P(DOM), P(None, DOM))
    return jax.shard_map(
        body,
        mesh=split,
        in_specs=placed,
        out_specs=(P(DOM, None), P(DOM, None, None), P()),
        check_vma=False,
    )
```

profile of v0, /device:TPU:32, one launch (start us, length us, event | category | flops | bytes accessed | tf_op | source)
XLA Modules:
  0.0 332.5 jit_solution(10021585373992793412)
XLA Ops:
  7.4 0.7 fusion.80
  8.1 0.8 cosine_bitcast_fusion.1
  8.9 1.3 copy_convert_fusion
  10.2 1.1 add_divide_fusion.1
  11.3 1.4 multiply_convert_fusion.1
  12.6 0.7 copy.32
  13.4 0.7 reshape.486
  14.1 2.1 fusion.26
  16.3 3.8 %copy.40 = bf16[32,8,1,14976]{3,0,2,1:T(8,128)(2,1)} copy(bf16[32,8,1,14976]{3,1,0,2:T(8,128)(2,1)S(1)} %fusion.26) | data formatting | bytes 15335424 | tf_op jit(solution)/shard_map/reshape;reshape | solution.py:20
  20.1 5.1 %all-to-all-start = ((bf16[8,32,1,14976]{3,1,2,0:T(8,128)(2,1)}), bf16[8,32,1,14976]{3,1,2,0:T(8,128)(2,1)}, u32[]{:S(2)}, u32[]{:S(2)}) async-start(bf16[8,32,1,14976]{3,1,2,0:T(8,128)(2,1)} %bitcast.71), calls=%async_computation | async-start | bytes 15335424 | tf_op jit(solution)/shard_map/all_to_all | solution.py:25
  25.2 0.7 all-gather.3.cloned.1.call-update
  25.9 150.9 %all-gather = s32[256,32,4]{1,2,0:T(4,128)S(1)} all-gather(s32[1,32,4]{1,2,0:T(4,128)S(1)} %add_bitcast_fusion), channel_id=1, replica_groups=mesh['dom_0'=4,'dom_1'=8,'dom_2'=4,'dom_3'=2] {'dom_0','dom_1','dom_2','..., dimensions={0}, use_global_device_ids=true | all-gather | bytes 131584 | tf_op jit(solution)/shard_map/all_gather | solution.py:103
  179.3 57.2 %scatter_custom_fusion = s32[8448]{0:T(1024)S(1)} fusion(s32[8192]{0:T(1024)S(1)} %bitcast.81, s32[8192]{0:T(1024)S(1)} %broadcast.1000, s32[]{:T(128)} %constant.270.clone.1), kind=kCustom, calls=%fused_computation.125 | custom fusion | flops 8192 | bytes 33796 | tf_op jit(solution)/shard_map/scatter-add | solution.py:108
  237.1 0.7 fusion.55
  237.8 4.4 %reduce_sum.94 = bf16[32,14976]{1,0:T(8,128)(2,1)S(1)} reduce(bf16[8,32,1,14976]{3,1,2,0:T(8,128)(2,1)} %all-to-all-done, bf16[]{:T(256)} %constant.286.clone.1), dimensions={0,2}, to_apply=%region_1.2 | reduce | flops 3354624 | bytes 8626178 | tf_op jit(solution)/shard_map/reduce_sum | solution.py:26
  242.7 1.4 reduce.7
  244.1 2.0 reshape.541
  246.1 7.1 %all-to-all-start.1 = ((bf16[32,2,7488]{2,1,0:T(2,128)(2,1)}), bf16[32,2,7488]{2,1,0:T(2,128)(2,1)}, u32[]{:S(2)}, u32[]{:S(2)}) async-start(bf16[32,2,7488]{2,1,0:T(2,128)(2,1)} %reshape.541), calls=%async_computation.1 | async-start | bytes 1933312 | tf_op jit(solution)/shard_map/all_to_all | solution.py:33
  253.2 15.0 %while.15 = (s32[]{:T(128)}, f32[7488]{0:T(1024)S(1)}, f32[]{:T(128)}, s32[]{:T(128)}, s32[]{:T(128)}, /*index=5*/s32[4,8192]{1,0:T(4,128)S(1)}, s32[8448]{0:T(1...) while((s32[]{:T(128)}, f32[7488]{0:T(1024)S(1)}, f32[]{:T(128)}, s32[]{:T(128)}, s32[]{:T(128)}, ...), condition=%wide.region_13.14_spmd, body=%wide.region_9.13_spmd.sunk | while | flops 46529604 | bytes 592063 | solution.py:123
  254.3 1.7 gather_fusion
  256.0 1.7 gather_fusion.1
  257.7 1.7 gather_fusion.2
  259.6 6.5 %fusion.100 = (f32[256]{0:T(256)S(1)}, f32[7488]{0:T(1024)S(1)}) fusion(f32[256]{0:T(256)S(1)} %get-tuple-element.240, f32[256]{0:T(256)S(1)} %sin.43, f32[7488]{0:T(1024)S(1)} %get-tuple-element.242, f32[256]{0:T(256)S(1)} %get-tuple-element.243, f32[7488]{0:T(1024)S(1)} %fusion.97, f32[256]{0:T(256)S(1)} %get-tuple-element.244, ...), kind=kLoop, calls=%fused_computation.7.clone.1 | loop fusion | flops 45998528 | bytes 156928 | tf_op jit(solution)/shard_map/while/body/reduce_sum | solution.py:120
  266.1 1.2 select_reduce_fusion.2
  268.2 1.2 convert_reduce_fusion
  270.0 10.2 %all-to-all-done.1 = bf16[32,2,7488]{2,1,0:T(2,128)(2,1)} async-done(((bf16[32,2,7488]{2,1,0:T(2,128)(2,1)}), bf16[32,2,7488]{2,1,0:T(2,128)(2,1)}, u32[]{:S(2)}, u32[]{:S(2)}) %all-to-all-start.1) | async-done | bytes 958496 | tf_op jit(solution)/shard_map/all_to_all | solution.py:33
  280.2 4.5 %reshape.542 = bf16[32,1,14976]{2,1,0:T(2,128)(2,1)S(1)} reshape(bf16[32,2,7488]{2,1,0:T(2,128)(2,1)} %all-to-all-done.1) | data formatting | bytes 1916928
  284.7 2.0 convert_reduce_fusion.1
  287.5 19.6 %copy.31 = bf16[256,2,7488]{0,2,1:T(8,128)(2,1)} copy(bf16[256,2,7488]{2,1,0:T(2,128)(2,1)} %all-gather.3.cloned.1.call-done) | data formatting | bytes 15335424 | tf_op jit(solution)/shard_map/all_gather | solution.py:79
  307.0 9.9 %convert_element_type.241 = f32[256,2,7488]{0,2,1:T(8,128)} convert(bf16[256,2,7488]{0,2,1:T(8,128)(2,1)} %copy.31) | non-fusion elementwise | flops 3833856 | bytes 23003136 | tf_op jit(solution)/shard_map/convert_element_type | solution.py:81
  317.0 6.5 %fusion.45 = f32[32,256]{1,0:T(8,128)S(1)} fusion(f32[256,2,7488]{0,2,1:T(8,128)} %convert_element_type.241, f32[32]{0:T(128)S(1)} %multiply_add_fusion, f32[32]{0:T(128)S(1)} %get-tuple-element.176, f32[32]{0:T(128)S(1)} %get-tuple-element.175, f32[7488]{0:T(1024)S(1)} %get-tuple-element.180, f32[32]{0:T(128)S(1)} %get-tuple-element.174, ...), kind=kOutput, calls=%fused_computation.71 | convolution fusion | flops 134936576 | bytes 15488768 | tf_op jit(solution)/shard_map/dot_general | solution.py:89
  323.6 2.0 fusion.32
  (51 shorter events, 5.5 us)
Async XLA Ops:
  7.2 7.0 %copy-start = (s32[32,1]{0,1:T(1,128)S(1)}, s32[32,1]{0,1:T(1,128)}, u32[]{:S(2)}) copy-start(s32[32,1]{0,1:T(1,128)} %param.9) | copy-start | bytes 388
  20.1 5.8 %copy-start.1 = (s32[2,32]{1,0:T(2,128)S(1)}, s32[2,32]{1,0:T(2,128)}, u32[]{:S(2)}) copy-start(s32[2,32]{1,0:T(2,128)} %param.11) | copy-start | bytes 772
  20.1 5.8 %copy-start.2 = (s32[32]{0:T(128)S(1)}, s32[32]{0:T(128)}, u32[]{:S(2)}) copy-start(s32[32]{0:T(128)} %param.10) | copy-start | bytes 388
  20.1 217.7 %all-to-all-start = ((bf16[8,32,1,14976]{3,1,2,0:T(8,128)(2,1)}), bf16[8,32,1,14976]{3,1,2,0:T(8,128)(2,1)}, u32[]{:S(2)}, u32[]{:S(2)}) async-start(bf16[8,32,1,14976]{3,1,2,0:T(8,128)(2,1)} %bitcast.71), calls=%async_computation | async-start | bytes 15335424 | tf_op jit(solution)/shard_map/all_to_all | solution.py:25
  25.2 262.3 %all-gather.3.cloned.1.call-start = ((), (), s32[]{:S(2)}) async-start(), calls=%async_computation.2 | async-start | bytes 7763456 | tf_op jit(solution)/shard_map/all_gather | solution.py:79
  246.1 34.1 %all-to-all-start.1 = ((bf16[32,2,7488]{2,1,0:T(2,128)(2,1)}), bf16[32,2,7488]{2,1,0:T(2,128)(2,1)}, u32[]{:S(2)}, u32[]{:S(2)}) async-start(bf16[32,2,7488]{2,1,0:T(2,128)(2,1)} %reshape.541), calls=%async_computation.1 | async-start | bytes 1933312 | tf_op jit(solution)/shard_map/all_to_all | solution.py:33
  307.0 16.5 %slice-start = ((s8[7667712]{0:T(1024)(128)(4,1)}), s8[3473408]{0:T(1024)(128)(4,1)S(1)}, s32[]{:S(2)}) async-start(s8[7667712]{0:T(1024)(128)(4,1)} %bitcast.69), calls=%async_computation.3 | async-start | bytes 6946816
  317.0 6.6 %slice-start.1 = ((s8[7667712]{0:T(1024)(128)(4,1)}), s8[4194304]{0:T(1024)(128)(4,1)S(1)}, s32[]{:S(2)}) async-start(s8[7667712]{0:T(1024)(128)(4,1)} %bitcast.69), calls=%async_computation.4 | async-start | bytes 8388608
Sparse Core Ops, SparseCore 0:
  29.7 133.0 all-gather.2
where the time goes:
time: 334 us; the launch traced here: 332 us
  blocking collectives  151 us (45%)
  other arithmetic  93.9 us (28%)
  local copies, waits for them, and re-layouts  38 us (11%)
  between operations  15 us (4%)
  starting transfers between devices  12.2 us (4%)
  waiting for transfers between devices  10.9 us (3%)
  matrix products  10.7 us (3%)
    all_gather x1, blocking collectives, body(): every = lax.all_gather(labels, DOM, axis=1, tiled=True)  151 us
    scatter-add x1, other arithmetic, body(): jnp.nonzero(chosen, size=total + member_rows, fill_value=0)[0]  57.2 us
    all_gather x1, local copies, waits for them, and re-layouts, body(): piece = lax.all_gather(references, DOM, axis=0, tiled=True)  19.6 us
    all_to_all x1, waiting for transfers between devices, sum_in_two_steps(): lax.all_to_all(own.astype(jnp.bfloat16), far, 0, 0, tiled=True)  10.2 us
    convert_element_type x1, other arithmetic, body(): p32 = piece.astype(jnp.float32)  9.95 us
    reduce_sum x2, other arithmetic, member_block(): wedge_sum = wedge_sum + jnp.sum(valid * jnp.sum(member_wedge, axis=1))  7.76 us
    all_to_all x1, starting transfers between devices, sum_in_two_steps(): lax.all_to_all(own.astype(jnp.bfloat16), far, 0, 0, tiled=True)  7.06 us
    unnamed x13, local copies, waits for them, and re-layouts  6.88 us
  transfers between devices with their start and end apart: 3, of which 1 were waited for; matrix products, arithmetic and copies ran while one was open for 28% of the time, Pallas kernels for 0%

commit v1 on v0

--- a/solution.py
+++ b/solution.py
@@ -100,7 +100,9 @@
         0,
     )
     labels = jnp.stack([cls, orientation, tilt_range[0], tilt_range[1]])
-    every = lax.all_gather(labels, DOM, axis=1, tiled=True)
+    every = jnp.concatenate(
+        lax.all_to_all(jnp.stack([labels] * lax.axis_size(DOM)), DOM, 0, 0), axis=1
+    )
     class_ids = jnp.arange(classes, dtype=jnp.int32)
     counts = jnp.sum((class_ids[:, None] == every[0][None, :]).astype(jnp.float32), axis=1)
     own_class = lax.axis_index(DOM) * owned + 0

time: 334 us -> 238 us (0.71)
  blocking collectives: 151 us -> 0 us
  waiting for transfers between devices: 10.9 us -> 45.2 us
  starting transfers between devices: 12.2 us -> 29.8 us
    all_gather x1 -> x0, blocking collectives: 151 us -> none  [body(): every = lax.all_gather(labels, DOM, axis=1, tiled=True)]
    all_to_all x1, waiting for transfers between devices: 0.01 us -> 25.6 us  [summed_on_arrival(): lax.all_to_all(tiles, axis, split_axis=0, concat_axis=0, tiled=True)]
    all_to_all x0 -> x1, starting transfers between devices: none -> 14.4 us  [body(): lax.all_to_all(jnp.stack([labels] * lax.axis_size(DOM)), DOM, 0, 0)]
    all_to_all x1, waiting for transfers between devices: 10.2 us -> 18.7 us  [sum_in_two_steps(): lax.all_to_all(own.astype(jnp.bfloat16), far, 0, 0, tiled=True)]
    all_to_all x1, starting transfers between devices: 7.06 us -> 10.5 us  [sum_in_two_steps(): lax.all_to_all(own.astype(jnp.bfloat16), far, 0, 0, tiled=True)]
    unnamed x13 -> x12, local copies, waits for them, and re-layouts: 6.88 us -> 7.87 us
  transfers between devices with their start and end apart: 3 -> 4, of which waited for: 1 -> 3; matrix products, arithmetic and copies ran while one was open for 28% -> 45% of each run, Pallas kernels for 0% -> 0%
where the time goes in v1:
time: 238 us; the launch traced here: 237 us
  other arithmetic  95.1 us (40%)
  waiting for transfers between devices  45.2 us (19%)
  local copies, waits for them, and re-layouts  40.1 us (17%)
  starting transfers between devices  29.8 us (13%)
  between operations  15 us (6%)
  matrix products  10.7 us (4%)
    scatter-add x1, other arithmetic, body(): jnp.nonzero(chosen, size=total + member_rows, fill_value=0)[0]  57.2 us
    all_to_all x1, waiting for transfers between devices, summed_on_arrival(): lax.all_to_all(tiles, axis, split_axis=0, concat_axis=0, tiled=True)  25.6 us
    all_gather x1, local copies, waits for them, and re-layouts, body(): piece = lax.all_gather(references, DOM, axis=0, tiled=True)  19.6 us
    all_to_all x1, waiting for transfers between devices, sum_in_two_steps(): lax.all_to_all(own.astype(jnp.bfloat16), far, 0, 0, tiled=True)  18.7 us
    all_to_all x1, starting transfers between devices, body(): lax.all_to_all(jnp.stack([labels] * lax.axis_size(DOM)), DOM, 0, 0)  14.4 us
    all_to_all x1, starting transfers between devices, sum_in_two_steps(): lax.all_to_all(own.astype(jnp.bfloat16), far, 0, 0, tiled=True)  10.5 us
    convert_element_type x1, other arithmetic, body(): p32 = piece.astype(jnp.float32)  9.95 us
    unnamed x12, local copies, waits for them, and re-layouts  7.87 us
  transfers between devices with their start and end apart: 4, of which 3 were waited for; matrix products, arithmetic and copies ran while one was open for 45% of the time, Pallas kernels for 0%

profile of v1, /device:TPU:32, one launch (start us, length us, event | category | flops | bytes accessed | tf_op | source)
XLA Modules:
  0.0 236.8 jit_solution(16448128113148729882)
XLA Ops:
  7.2 0.8 pad_add_fusion
  8.1 1.0 reshape.566
  9.0 14.4 %all-to-all-start.2 = ((s32[256,1,128]{2,1,0:T(1,128)}), s32[256,1,128]{2,1,0:T(1,128)S(1)}, u32[]{:S(2)}, u32[]{:S(2)}) async-start(s32[256,1,128]{2,1,0:T(1,128)} %reshape.566), calls=%async_computation.2 | async-start | bytes 262144 | tf_op jit(solution)/shard_map/all_to_all | solution.py:104
  24.1 0.8 cosine_bitcast_fusion.1
  25.1 1.3 copy_convert_fusion
  26.5 1.1 add_divide_fusion.1
  27.7 0.7 copy.30
  29.2 2.1 fusion.26
  31.3 3.9 %copy.38 = bf16[32,8,1,14976]{3,0,2,1:T(8,128)(2,1)} copy(bf16[32,8,1,14976]{3,1,0,2:T(8,128)(2,1)S(1)} %fusion.26) | data formatting | bytes 15335424 | tf_op jit(solution)/shard_map/reshape;reshape | solution.py:20
  35.4 4.9 %all-to-all-start = ((bf16[8,32,1,14976]{3,1,2,0:T(8,128)(2,1)}), bf16[8,32,1,14976]{3,1,2,0:T(8,128)(2,1)}, u32[]{:S(2)}, u32[]{:S(2)}) async-start(bf16[8,32,1,14976]{3,1,2,0:T(8,128)(2,1)} %bitcast.63), calls=%async_computation | async-start | bytes 15335424 | tf_op jit(solution)/shard_map/all_to_all | solution.py:25
  41.6 0.9 reduce.17
  42.8 1.4 slice_reduce_fusion.2
  46.0 57.2 %scatter_custom_fusion = s32[8448]{0:T(1024)S(1)} fusion(s32[8192]{0:T(1024)S(1)} %bitcast.69, s32[8192]{0:T(1024)S(1)} %broadcast.1003, s32[]{:T(128)} %constant.270.clone.1), kind=kCustom, calls=%fused_computation.126 | custom fusion | flops 8192 | bytes 33796 | tf_op jit(solution)/shard_map/scatter-add | solution.py:110
  104.5 25.6 %all-to-all-done = bf16[8,32,1,14976]{3,1,2,0:T(8,128)(2,1)} async-done(((bf16[8,32,1,14976]{3,1,2,0:T(8,128)(2,1)}), bf16[8,32,1,14976]{3,1,2,0:T(8,128)(2,1)}, u32[]{:S(2)}, u32[]{:S(2)}) %all-to-all-start) | async-done | bytes 7667744 | tf_op jit(solution)/shard_map/all_to_all | solution.py:25
  130.2 4.4 %reduce_sum.94 = bf16[32,14976]{1,0:T(8,128)(2,1)S(1)} reduce(bf16[8,32,1,14976]{3,1,2,0:T(8,128)(2,1)} %all-to-all-done, bf16[]{:T(256)} %constant.286.clone.1), dimensions={0,2}, to_apply=%region_1.2 | reduce | flops 3354624 | bytes 8626178 | tf_op jit(solution)/shard_map/reduce_sum | solution.py:26
  135.1 1.4 reduce.16
  136.4 2.0 reshape.564
  138.5 10.5 %all-to-all-start.1 = ((bf16[32,2,7488]{2,1,0:T(2,128)(2,1)}), bf16[32,2,7488]{2,1,0:T(2,128)(2,1)}, u32[]{:S(2)}, u32[]{:S(2)}) async-start(bf16[32,2,7488]{2,1,0:T(2,128)(2,1)} %reshape.564), calls=%async_computation.1 | async-start | bytes 1933312 | tf_op jit(solution)/shard_map/all_to_all | solution.py:33
  149.0 15.0 %while.15 = (s32[]{:T(128)}, f32[7488]{0:T(1024)S(1)}, f32[]{:T(128)}, s32[]{:T(128)}, s32[]{:T(128)}, /*index=5*/s32[4,8192]{1,0:T(4,128)S(1)}, s32[8448]{0:T(1...) while((s32[]{:T(128)}, f32[7488]{0:T(1024)S(1)}, f32[]{:T(128)}, s32[]{:T(128)}, s32[]{:T(128)}, ...), condition=%wide.region_13.14_spmd, body=%wide.region_9.13_spmd.sunk | while | flops 46529604 | bytes 592063 | solution.py:125
  150.0 1.7 gather_fusion
  151.8 1.7 gather_fusion.1
  153.5 1.7 gather_fusion.2
  155.3 6.5 %fusion.102 = (f32[256]{0:T(256)S(1)}, f32[7488]{0:T(1024)S(1)}) fusion(f32[256]{0:T(256)S(1)} %get-tuple-element.243, f32[256]{0:T(256)S(1)} %sin.43, f32[7488]{0:T(1024)S(1)} %get-tuple-element.245, f32[256]{0:T(256)S(1)} %get-tuple-element.246, f32[7488]{0:T(1024)S(1)} %fusion.99, f32[256]{0:T(256)S(1)} %get-tuple-element.247, ...), kind=kLoop, calls=%fused_computation.7.clone.1 | loop fusion | flops 45998528 | bytes 156928 | tf_op jit(solution)/shard_map/while/body/reduce_sum | solution.py:122
  161.9 1.2 select_reduce_fusion.2
  164.1 1.2 convert_reduce_fusion
  165.9 18.7 %all-to-all-done.1 = bf16[32,2,7488]{2,1,0:T(2,128)(2,1)} async-done(((bf16[32,2,7488]{2,1,0:T(2,128)(2,1)}), bf16[32,2,7488]{2,1,0:T(2,128)(2,1)}, u32[]{:S(2)}, u32[]{:S(2)}) %all-to-all-start.1) | async-done | bytes 958496 | tf_op jit(solution)/shard_map/all_to_all | solution.py:33
  184.6 4.5 %reshape.565 = bf16[32,1,14976]{2,1,0:T(2,128)(2,1)S(1)} reshape(bf16[32,2,7488]{2,1,0:T(2,128)(2,1)} %all-to-all-done.1) | data formatting | bytes 1916928
  189.1 2.0 convert_reduce_fusion.1
  191.9 19.6 %copy.29 = bf16[256,2,7488]{0,2,1:T(8,128)(2,1)} copy(bf16[256,2,7488]{2,1,0:T(2,128)(2,1)} %all-gather.2.cloned.1.call-done) | data formatting | bytes 15335424 | tf_op jit(solution)/shard_map/all_gather | solution.py:79
  211.4 9.9 %convert_element_type.242 = f32[256,2,7488]{0,2,1:T(8,128)} convert(bf16[256,2,7488]{0,2,1:T(8,128)(2,1)} %copy.29) | non-fusion elementwise | flops 3833856 | bytes 23003136 | tf_op jit(solution)/shard_map/convert_element_type | solution.py:81
  221.4 6.5 %fusion.45 = f32[32,256]{1,0:T(8,128)S(1)} fusion(f32[256,2,7488]{0,2,1:T(8,128)} %convert_element_type.242, f32[32]{0:T(128)S(1)} %multiply_add_fusion, f32[32]{0:T(128)S(1)} %get-tuple-element.179, f32[32]{0:T(128)S(1)} %get-tuple-element.178, f32[7488]{0:T(1024)S(1)} %get-tuple-element.183, f32[32]{0:T(128)S(1)} %get-tuple-element.177, ...), kind=kOutput, calls=%fused_computation.71 | convolution fusion | flops 134936576 | bytes 15488768 | tf_op jit(solution)/shard_map/dot_general | solution.py:89
  228.0 2.0 fusion.32
  (55 shorter events, 9.1 us)
Async XLA Ops:
  7.2 22.0 %copy-start.1 = (s32[32,1]{0,1:T(1,128)S(1)}, s32[32,1]{0,1:T(1,128)}, u32[]{:S(2)}) copy-start(s32[32,1]{0,1:T(1,128)} %param.9) | copy-start | bytes 388
  7.2 20.4 %copy-start = (bf16[32,2,7488]{2,1,0:T(2,128)(2,1)S(1)}, bf16[32,2,7488]{2,1,0:T(2,128)(2,1)}, u32[]{:S(2)}) copy-start(bf16[32,2,7488]{2,1,0:T(2,128)(2,1)} %param.7) | copy-start | bytes 2875396
  9.0 26.4 %all-to-all-start.2 = ((s32[256,1,128]{2,1,0:T(1,128)}), s32[256,1,128]{2,1,0:T(1,128)S(1)}, u32[]{:S(2)}, u32[]{:S(2)}) async-start(s32[256,1,128]{2,1,0:T(1,128)} %reshape.566), calls=%async_computation.2 | async-start | bytes 262144 | tf_op jit(solution)/shard_map/all_to_all | solution.py:104
  35.4 94.7 %all-to-all-start = ((bf16[8,32,1,14976]{3,1,2,0:T(8,128)(2,1)}), bf16[8,32,1,14976]{3,1,2,0:T(8,128)(2,1)}, u32[]{:S(2)}, u32[]{:S(2)}) async-start(bf16[8,32,1,14976]{3,1,2,0:T(8,128)(2,1)} %bitcast.63), calls=%async_computation | async-start | bytes 15335424 | tf_op jit(solution)/shard_map/all_to_all | solution.py:25
  40.3 151.5 %all-gather.2.cloned.1.call-start = ((), (), s32[]{:S(2)}) async-start(), calls=%async_computation.3 | async-start | bytes 7763456 | tf_op jit(solution)/shard_map/all_gather | solution.py:79
  138.5 46.1 %all-to-all-start.1 = ((bf16[32,2,7488]{2,1,0:T(2,128)(2,1)}), bf16[32,2,7488]{2,1,0:T(2,128)(2,1)}, u32[]{:S(2)}, u32[]{:S(2)}) async-start(bf16[32,2,7488]{2,1,0:T(2,128)(2,1)} %reshape.564), calls=%async_computation.1 | async-start | bytes 1933312 | tf_op jit(solution)/shard_map/all_to_all | solution.py:33
  211.4 16.5 %slice-start = ((s8[7667712]{0:T(1024)(128)(4,1)}), s8[3473408]{0:T(1024)(128)(4,1)S(1)}, s32[]{:S(2)}) async-start(s8[7667712]{0:T(1024)(128)(4,1)} %bitcast.61), calls=%async_computation.4 | async-start | bytes 6946816
  221.4 6.6 %slice-start.1 = ((s8[7667712]{0:T(1024)(128)(4,1)}), s8[4194304]{0:T(1024)(128)(4,1)S(1)}, s32[]{:S(2)}) async-start(s8[7667712]{0:T(1024)(128)(4,1)} %bitcast.61), calls=%async_computation.5 | async-start | bytes 8388608
Sparse Core Ops, SparseCore 0:
  44.9 144.2 all-gather.1
